TPU v7x, 32 devices: a whole 2x2x4 slice. The times are simulated.
32 devices in a mesh: batch: 4 (over y, x), heads: 8 (over z, core).
Axes of the slice: x: 2, y: 2, z: 4, core: 2. Of those that a mesh axis runs over, the one named last changes fastest.
Arguments:
- draft_ids: int32 [192, 8], P('batch'), may hold values from 0 to 50279
- accepted: int32 [192], P('batch'), may hold values from 1 to 8
- embedding: bfloat16 [50280, 2560], P(None, 'heads'), may hold values from -6 to 6
- norm_gain: float32 [2, 2560], replicated, may hold values from 0.5 to 1.5
- w_zx: bfloat16 [2, 2560, 8, 128], P(None, None, 'heads'), may hold values from -0.125 to 0.125
- w_dt: bfloat16 [2, 2560, 8], P(None, None, 'heads'), may hold values from -0.125 to 0.125
- w_bc: bfloat16 [2, 2560, 256], P(None, None, 'heads'), may hold values from -0.125 to 0.125
- dt_bias: float32 [2, 8], P(None, 'heads'), may hold values from -4 to -1
- decay_rate: float32 [2, 8], P(None, 'heads'), may hold values from 1 to 16
- skip_weight: float32 [2, 8], P(None, 'heads'), may hold values from 0.5 to 1.5
- conv_x_w: bfloat16 [2, 4, 512], P(None, None, 'heads'), may hold values from -3 to 3
- conv_x_b: bfloat16 [2, 512], P(None, 'heads'), may hold values from -3 to 3
- conv_bc_w: bfloat16 [2, 4, 256], P(None, None, 'heads'), may hold values from -3 to 3
- conv_bc_b: bfloat16 [2, 256], P(None, 'heads'), may hold values from -3 to 3
- gate_gain: float32 [2, 512], P(None, 'heads'), may hold values from 0.5 to 1.5
- out_w: bfloat16 [2, 512, 2560], P(None, 'heads'), may hold values from -0.375 to 0.375
- ssm_state: float32 [2, 192, 8, 64, 128], P(None, 'batch', 'heads'), may hold values from -1.6 to 1.6
- conv_x_state: bfloat16 [2, 192, 3, 512], P(None, 'batch', None, 'heads'), may hold values from -6 to 6
- conv_bc_state: bfloat16 [2, 192, 3, 256], P(None, 'batch', None, 'heads'), may hold values from -6 to 6
Outputs:
- hidden_out: bfloat16 [1536, 2560], P('batch', 'heads')
- new_ssm: float32 [2, 192, 8, 64, 128], P(None, 'batch', 'heads')
- new_conv_x: bfloat16 [2, 192, 3, 512], P(None, 'batch', None, 'heads')
- new_conv_bc: bfloat16 [2, 192, 3, 256], P(None, 'batch', None, 'heads')
Inputs may be any that keep to these rules, and one draw needn't show every extreme that they name: `accepted`: the number of a sequence's draft tokens that are kept, counted from the first.
All inputs are finite; a program needn't handle non-finite values.
Results may differ from a plain program's by a relative error of at most 0.015.
Values may be sent and summed in bfloat16 or wider, within the bound.
A program may use at most 128 MiB of HBM per device.

v0:
```python
import jax
import jax.numpy as jnp
from jax import lax
from jax.sharding import PartitionSpec as P

LAYERS = 2
EPS = 1e-05


def rms_scale(total, count):
    return lax.rsqrt(total / count + EPS)


def convolve(window, weight, bias, count):
    weight = weight.astype(jnp.float32)
    acc = window[:, 0:count] * weight[0]
    for k in range(1, weight.shape[0]):
        acc = acc + window[:, k : k + count] * weight[k]
    return jax.nn.silu(acc + bias.astype(jnp.float32))


def keep_rows(window, accepted, kept_rows):
    last_start = window.shape[1] - kept_rows
    kept = window[:, 1 : 1 + kept_rows]
    for start in range(2, last_start + 1):
        kept = jnp.where(
            (accepted == start)[:, None, None], window[:, start : start + kept_rows], kept
        )
    return kept


def recur(decay, step, values, bmat, cmat, skip, state, accepted):
    kept = state
    outputs = []
    for t in range(values.shape[1]):
        state = (
            decay[:, t, None, None] * state
            + (step[:, t, None] * values[:, t])[:, :, None] * bmat[:, t, None, :]
        )
        outputs.append(jnp.sum(state * cmat[:, t, None, :], axis=-1) + skip * values[:, t])
        kept = jnp.where((accepted == t + 1)[:, None, None], state, kept)
    return (jnp.stack(outputs, 1), kept)


def spread_terms(u_rows, scale, weight):
    product = lax.dot_general(
        weight, u_rows, (((0,), (1,)), ((), ())), preferred_element_type=jnp.float32
    )
    return product * scale[None, :]


def token_scale(local_sq, inner):
    return rms_scale(lax.psum(local_sq, "heads"), inner)


def local(
    draft_ids,
    accepted,
    embedding,
    norm_gain,
    w_zx,
    w_dt,
    w_bc,
    dt_bias,
    decay_rate,
    skip_weight,
    conv_x_w,
    conv_x_b,
    conv_bc_w,
    conv_bc_b,
    gate_gain,
    out_w,
    ssm_state,
    conv_x_state,
    conv_bc_state,
):
    seq_rows, draft = draft_ids.shape
    heads_here = w_zx.shape[2]
    width = w_zx.shape[3] // 2
    local_inner = heads_here * width
    own_cols = embedding.shape[1]
    model = own_cols * lax.axis_size("heads")
    inner = local_inner * lax.axis_size("heads")
    bc_here = w_bc.shape[2]
    kernel = conv_x_w.shape[1]
    recur_heads = jax.vmap(recur, in_axes=(2, 2, 2, None, None, 0, 1, None), out_axes=(2, 1))
    whole_bc = (
        lax.all_gather(w_bc, "heads", axis=2, tiled=True),
        lax.all_gather(conv_bc_w, "heads", axis=2, tiled=True),
        lax.all_gather(conv_bc_b, "heads", axis=1, tiled=True),
        lax.all_gather(conv_bc_state, "heads", axis=3, tiled=True),
    )
    saved_state, saved_x, saved_bc = ([], [], [])

    def mixer(layer, stream):
        value = stream.astype(jnp.float32)
        normed = (
            value * rms_scale(jnp.sum(value * value, -1, keepdims=True), model) * norm_gain[layer]
        ).astype(jnp.bfloat16)
        zx = jnp.dot(
            normed, w_zx[layer].reshape(model, -1), preferred_element_type=jnp.float32
        ).astype(jnp.bfloat16)
        zx = zx.reshape(seq_rows, draft, heads_here, 2, width)
        gate_z = zx[:, :, :, 0].astype(jnp.float32)
        values = zx[:, :, :, 1].reshape(seq_rows, draft, local_inner)
        dt_raw = (
            jnp.dot(normed, w_dt[layer], preferred_element_type=jnp.float32)
            .astype(jnp.bfloat16)
            .reshape(seq_rows, draft, heads_here)
        )
        bc = (
            jnp.dot(normed, whole_bc[0][layer], preferred_element_type=jnp.float32)
            .astype(jnp.bfloat16)
            .reshape(seq_rows, draft, -1)
        )
        window_bc = jnp.concatenate([whole_bc[3][layer], bc], axis=1)
        bcc = convolve(
            window_bc.astype(jnp.float32), whole_bc[1][layer], whole_bc[2][layer], draft
        ).astype(jnp.bfloat16)
        kept_bc = keep_rows(window_bc, accepted, kernel - 1)
        bcc = lax.optimization_barrier(bcc).astype(jnp.float32)
        kept_bc = lax.dynamic_slice_in_dim(kept_bc, lax.axis_index("heads") * bc_here, bc_here, 2)
        states = bcc.shape[2] // 2
        bmat = bcc[..., :states]
        cmat = bcc[..., states:]
        window_x = jnp.concatenate([conv_x_state[layer], values], axis=1)
        xc = convolve(
            window_x.astype(jnp.float32), conv_x_w[layer], conv_x_b[layer], draft
        ).reshape(seq_rows, draft, heads_here, width)
        step = jax.nn.softplus(dt_raw.astype(jnp.float32) + dt_bias[layer])
        decay = jnp.exp(-step * decay_rate[layer])
        outputs, kept = recur_heads(
            decay, step, xc, bmat, cmat, skip_weight[layer], ssm_state[layer], accepted
        )
        saved_state.append(kept)
        saved_x.append(keep_rows(window_x, accepted, kernel - 1))
        saved_bc.append(kept_bc)
        gated = outputs * jax.nn.silu(gate_z)
        local_sq = jnp.sum(gated * gated, axis=(2, 3)).reshape(-1)
        u_rows = (
            (gated.reshape(seq_rows, draft, local_inner) * gate_gain[layer])
            .astype(jnp.bfloat16)
            .reshape(-1, local_inner)
        )
        return (u_rows, local_sq)

    part = embedding[draft_ids.reshape(-1)]
    stream = lax.all_gather(part, "heads", axis=1, tiled=True)
    where_cols = lax.axis_index("heads") * own_cols
    result = part
    for layer in range(LAYERS):
        u_rows, local_sq = mixer(layer, stream)
        scale = token_scale(local_sq, inner)
        if layer + 1 < LAYERS:
            term = (
                jnp.dot(u_rows, out_w[layer], preferred_element_type=jnp.float32) * scale[:, None]
            )
            total = lax.psum(term, "heads")
            stream = (stream.astype(jnp.float32) + total).astype(jnp.bfloat16)
        else:
            mine = lax.psum_scatter(
                spread_terms(u_rows, scale, out_w[layer]), "heads", scatter_dimension=0, tiled=True
            )
            own_stream = lax.dynamic_slice_in_dim(stream, where_cols, own_cols, 1)
            result = (own_stream.astype(jnp.float32) + mine.T).astype(jnp.bfloat16)
    return (result, jnp.stack(saved_state), jnp.stack(saved_x), jnp.stack(saved_bc))


def solution(mesh):
    placed = (
        P("batch", None),
        P("batch"),
        P(None, "heads"),
        P(),
        P(None, None, "heads", None),
        P(None, None, "heads"),
        P(None, None, "heads"),
        P(None, "heads"),
        P(None, "heads"),
        P(None, "heads"),
        P(None, None, "heads"),
        P(None, "heads"),
        P(None, None, "heads"),
        P(None, "heads"),
        P(None, "heads"),
        P(None, "heads", None),
        P(None, "batch", "heads", None, None),
        P(None, "batch", None, "heads"),
        P(None, "batch", None, "heads"),
    )
    return jax.shard_map(
        local,
        mesh=mesh,
        in_specs=placed,
        out_specs=(
            P("batch", "heads"),
            P(None, "batch", "heads", None, None),
            P(None, "batch", None, "heads"),
            P(None, "batch", None, "heads"),
        ),
        check_vma=False,
    )
```

profile of v0, /device:TPU:0, one launch (start us, length us, event | category | flops | bytes accessed | tf_op | source)
XLA Modules:
  0.0 371.8 jit_solution(4346947506731001234)
XLA Ops:
  7.2 43.7 %copy.113 = bf16[50280,320]{1,0:T(8,128)(2,1)} copy(bf16[50280,320]{0,1:T(8,128)(2,1)} %param.21) | data formatting | bytes 64358400 | tf_op args[2]
  51.2 7.8 %gather_fusion = bf16[384,320]{1,0:T(8,128)(2,1)S(1)} fusion(bf16[50280,320]{1,0:T(8,128)(2,1)} %copy.113, s32[1024]{0:T(1024)S(1)} %pad_clamp_fusion), kind=kCustom, calls=%fused_computation | custom fusion | bytes 493056 | tf_op jit(solution)/shard_map/gather | solution.py:147
  60.8 16.7 %all_gather.16 = bf16[2,48,3,256]{1,3,2,0:T(8,128)(2,1)S(1)} all-gather(bf16[2,48,3,32]{1,3,2,0:T(8,128)(2,1)S(1)} %copy-done.48), channel_id=1, replica_groups=mesh['batch'=4,'heads'=8] {'heads'}, dimensions={3}, use_global_device_ids=true | all-gather | bytes 165888 | tf_op jit(solution)/shard_map/all_gather | solution.py:91
  77.9 15.1 %all_gather.18 = bf16[2,4,256]{1,0,2:T(2,128)(2,1)S(1)} all-gather(bf16[2,4,32]{1,0,2:T(2,128)(2,1)S(1)} %copy.118), channel_id=1, replica_groups=mesh['batch'=4,'heads'=8] {'heads'}, dimensions={2}, use_global_device_ids=true | all-gather | bytes 4608 | tf_op jit(solution)/shard_map/all_gather | solution.py:89
  93.0 12.0 %all-gather.1 = bf16[8,32,2]{1,2,0:T(2,128)(2,1)S(1)} all-gather(bf16[1,32,2]{1,2,0:T(2,128)(2,1)S(1)} %bitcast.580), channel_id=1, replica_groups=mesh['batch'=4,'heads'=8] {'heads'}, dimensions={0}, use_global_device_ids=true | all-gather | bytes 1152 | tf_op jit(solution)/shard_map/all_gather | solution.py:90
  107.1 2.9 slice_reduce_fusion.7
  111.3 2.7 copy.115
  119.7 7.5 %all-gather.5.cloned.1.call-done = bf16[2,2560,256]{1,2,0:T(8,128)(2,1)} async-done(((bf16[2,2560,32]{1,2,0:T(8,128)(2,1)}), bf16[2,2560,256]{1,2,0:T(8,128)(2,1)}) %all-gather.5.cloned.1.call-update) | async-done | bytes 2621456 | tf_op jit(solution)/shard_map/all_gather | solution.py:88
  127.2 2.0 fusion.15
  131.2 4.1 %multiply_add_fusion.8 = (f32[1,48,64,128]{3,2,1,0:T(8,128)S(1)}, f32[1,48,64,128]{3,2,1,0:T(8,128)S(1)}, f32[48,64]{1,0:T(8,128)S(1)}, f32[48,64]{1,0:T(8,128)S(1)}) fusion(f32[48,128]{1,0:T(8,128)S(1)} %bitcast.537, f32[48,64]{1,0:T(8,128)S(1)} %get-tuple-element.186, f32[48]{0:T(128)S(1)} %get-tuple-element.237, f32[48,128]{1,0:T(8,128)S(1)} %bitcast.525, ...), kind=kLoop, calls=%fused_computation.43 | loop fusion | flops 7464960 | bytes 4977600 | tf_op jit(solution)/shard_map/vmap()/add | solution.py:37
  136.0 1.6 multiply_reduce_fusion.12
  139.5 3.7 multiply_reduce_fusion.8
  145.9 15.0 %psum.21 = f32[384]{0:T(512)S(1)} all-reduce(f32[384]{0:T(512)S(1)} %reshape.2511), channel_id=1, replica_groups=mesh['batch'=4,'heads'=8] {'heads'}, use_global_device_ids=true, to_apply=%region_10.11 | all-reduce | flops 384 | bytes 3072 | tf_op jit(solution)/shard_map/psum | solution.py:53
  160.9 3.5 convolution_multiply_fusion.1
  165.6 2.9 slice_reduce_fusion.3
  168.5 85.9 %all-reduce.2.cloned.1.call-done = f32[384,2560]{1,0:T(8,128)} async-done(((f32[384,2560]{1,0:T(8,128)}), f32[384,2560]{1,0:T(8,128)}) %all-reduce.2.cloned.1.call-update) | async-done | bytes 3932176 | tf_op jit(solution)/shard_map/psum | solution.py:158
  254.3 2.9 fusion.1
  264.7 2.1 fusion.14
  268.8 4.1 %multiply_add_fusion.2 = (f32[1,48,64,128]{3,2,1,0:T(8,128)S(1)}, f32[1,48,64,128]{3,2,1,0:T(8,128)S(1)}, f32[48,64]{1,0:T(8,128)S(1)}, f32[48,64]{1,0:T(8,128)S(1)}) fusion(f32[48,128]{1,0:T(8,128)S(1)} %bitcast.551, f32[48,64]{1,0:T(8,128)S(1)} %get-tuple-element.160, f32[48]{0:T(128)S(1)} %get-tuple-element.51, f32[48,128]{1,0:T(8,128)S(1)} %bitcast.528, ...), kind=kLoop, calls=%fused_computation.29 | loop fusion | flops 7464960 | bytes 4977600 | tf_op jit(solution)/shard_map/vmap()/add | solution.py:37
  274.2 1.6 multiply_reduce_fusion.4
  279.5 3.7 multiply_reduce_fusion
  286.7 1.9 constant_dynamic-update-slice_fusion.16
  290.3 15.7 %psum.23 = f32[384]{0:T(512)S(1)} all-reduce(f32[384]{0:T(512)S(1)} %reshape.2516), channel_id=1, replica_groups=mesh['batch'=4,'heads'=8] {'heads'}, use_global_device_ids=true, to_apply=%region_22.23 | all-reduce | flops 384 | bytes 3072 | tf_op jit(solution)/shard_map/psum | solution.py:53
  307.1 3.5 fusion
  310.6 5.6 %copy.139 = f32[2560,384]{1,0:T(8,128)} copy(f32[2560,384]{0,1:T(8,128)} %fusion) | data formatting | bytes 7864320
  317.5 1.7 fusion.105
  319.1 1.4 fusion.119
  322.0 9.0 %select_select_fusion.1 = f32[1,48,1,64,128]{4,3,2,1,0:T(8,128)} fusion(f32[2,48,1,64,128]{4,3,2,1,0:T(8,128)S(1)} %copy-done.1, f32[48,128]{1,0:T(8,128)} %bitcast.536, f32[48,64]{1,0:T(8,128)} %copy-done.34, f32[48,128]{1,0:T(8,128)} %bitcast.534, f32[48,64]{1,0:T(8,128)} %copy-done.35, f32[48,128]{1,0:T(8,128)} %bitcast.532, f32[48,64]{1,0:T(8,128)} %copy-done.33, ...), kind=kLoop, calls=%fused_computation.22 | loop fusion | flops 12582912 | bytes 3442560 | tf_op jit(solution)/shard_map/vmap(jit(_where))/select_n | solution.py:41
  334.7 1.4 pad_maximum_fusion.5
  336.1 8.2 %select_select_fusion = f32[1,48,1,64,128]{4,3,2,1,0:T(8,128)S(1)} fusion(f32[2,48,1,64,128]{4,3,2,1,0:T(8,128)S(1)} %copy-done.1, f32[48,128]{1,0:T(8,128)} %bitcast.550, f32[48,64]{1,0:T(8,128)} %copy-done.40, f32[48,128]{1,0:T(8,128)} %bitcast.548, f32[48,64]{1,0:T(8,128)} %copy-done.42, f32[48,128]{1,0:T(8,128)} %bitcast.546, f32[48,64]{1,0:T(8,128)} %copy-done.41, ...), kind=kLoop, calls=%fused_computation.21 | loop fusion | flops 12582912 | bytes 3442560 | tf_op jit(solution)/shard_map/vmap(jit(_where))/select_n | solution.py:41
  344.4 1.9 pad_maximum_fusion
  346.3 15.7 %reduce-scatter.4.cloned.1.call-done = f32[320,384]{1,0:T(8,128)} async-done(((f32[2560,384]{1,0:T(8,128)}), f32[320,384]{1,0:T(8,128)}) %reduce-scatter.4.cloned.1.call-update) | async-done | bytes 491536
  (275 shorter events, 48.5 us)
Async XLA Ops:
  7.2 43.8 %copy-start.73 = (s32[48,8]{0,1:T(8,128)S(1)}, s32[48,8]{0,1:T(8,128)}, u32[]{:S(2)}) copy-start(s32[48,8]{0,1:T(8,128)} %param.19) | copy-start | bytes 4612
  7.2 104.1 %all-gather.7.cloned.1.call-start = ((), (), s32[]{:S(2)}) async-start(), calls=%async_computation.3 | async-start | bytes 2211840 | tf_op jit(solution)/shard_map/all_gather | solution.py:148
  59.0 18.7 %copy-start.75 = (bf16[2,4,32]{2,1,0:T(4,128)(2,1)S(1)}, bf16[2,4,32]{2,1,0:T(4,128)(2,1)}, u32[]{:S(2)}) copy-start(bf16[2,4,32]{2,1,0:T(4,128)(2,1)} %param.31) | copy-start | bytes 1540
  59.0 34.0 %copy-start.82 = (bf16[2,32]{1,0:T(2,128)(2,1)S(1)}, bf16[2,32]{1,0:T(2,128)(2,1)}, u32[]{:S(2)}) copy-start(bf16[2,32]{1,0:T(2,128)(2,1)} %param.32) | copy-start | bytes 388
  59.0 46.1 %copy-start.77 = (f32[2,1]{0,1:T(1,128)S(1)}, f32[2,1]{0,1:T(1,128)}, u32[]{:S(2)}) copy-start(f32[2,1]{0,1:T(1,128)} %param.26) | copy-start | bytes 28
  59.0 46.7 %copy-start.78 = (f32[2,1]{0,1:T(1,128)S(1)}, f32[2,1]{0,1:T(1,128)}, u32[]{:S(2)}) copy-start(f32[2,1]{0,1:T(1,128)} %param.27) | copy-start | bytes 28
  59.1 47.3 %copy-start.79 = (f32[2,1]{0,1:T(1,128)S(1)}, f32[2,1]{0,1:T(1,128)}, u32[]{:S(2)}) copy-start(f32[2,1]{0,1:T(1,128)} %param.28) | copy-start | bytes 28
  59.1 47.8 %copy-start.55 = (f32[2,2560]{1,0:T(2,128)S(1)}, f32[2,2560]{1,0:T(2,128)}, u32[]{:S(2)}) copy-start(f32[2,2560]{1,0:T(2,128)} %param.22) | copy-start | bytes 61444
  60.0 50.1 %copy-start.80 = (bf16[2,64]{1,0:T(2,128)(2,1)S(1)}, bf16[2,64]{1,0:T(2,128)(2,1)}, u32[]{:S(2)}) copy-start(bf16[2,64]{1,0:T(2,128)(2,1)} %param.30) | copy-start | bytes 772
  60.0 50.1 %copy-start.81 = (f32[2,64]{1,0:T(2,128)S(1)}, f32[2,64]{1,0:T(2,128)}, u32[]{:S(2)}) copy-start(f32[2,64]{1,0:T(2,128)} %param.33) | copy-start | bytes 1540
  60.0 51.2 %copy-start.76 = (bf16[2,4,64]{2,1,0:T(4,128)(2,1)S(1)}, bf16[2,4,64]{2,1,0:T(4,128)(2,1)}, u32[]{:S(2)}) copy-start(bf16[2,4,64]{2,1,0:T(4,128)(2,1)} %param.29) | copy-start | bytes 3076
  60.0 51.2 %copy-start.47 = (bf16[2,48,3,64]{3,1,2,0:T(8,128)(2,1)S(1)}, bf16[2,48,3,64]{3,1,2,0:T(8,128)(2,1)}, u32[]{:S(2)}) copy-start(bf16[2,48,3,64]{3,1,2,0:T(8,128)(2,1)} %param.36) | copy-start | bytes 110596
  60.0 67.2 %all-gather.5.cloned.1.call-start = ((), (), s32[]{:S(2)}) async-start(), calls=%async_computation.1 | async-start | bytes 2949120 | tf_op jit(solution)/shard_map/all_gather | solution.py:88
  60.8 193.6 %all-reduce.2.cloned.1.call-start = ((), (), s32[]{:S(2)}) async-start(), calls=%async_computation.2 | async-start | bytes 7864320 | tf_op jit(solution)/shard_map/psum | solution.py:158
  77.8 51.5 %copy-start.10 = (bf16[48,3,256]{2,1,0:T(4,128)(2,1)}, bf16[48,3,256]{2,1,0:T(4,128)(2,1)S(1)}, u32[]{:S(2)}) copy-start(bf16[48,3,256]{2,1,0:T(4,128)(2,1)S(1)} %copy.117) | copy-start | bytes 221188
  111.3 149.2 %copy-start.17 = (bf16[48,3,64]{2,0,1:T(8,128)(2,1)}, bf16[48,3,64]{2,0,1:T(8,128)(2,1)S(1)}, u32[]{:S(2)}) copy-start(bf16[48,3,64]{2,0,1:T(8,128)(2,1)S(1)} %get-tuple-element.193) | copy-start | bytes 55300
  119.3 16.7 %copy-start.56 = (f32[48]{0:T(128)}, f32[48]{0:T(128)S(1)}, u32[]{:S(2)}) copy-start(f32[48]{0:T(128)S(1)} %get-tuple-element.236) | copy-start | bytes 580
  119.3 20.1 %copy-start.66 = (f32[48]{0:T(128)}, f32[48]{0:T(128)S(1)}, u32[]{:S(2)}) copy-start(f32[48]{0:T(128)S(1)} %get-tuple-element.238) | copy-start | bytes 580
  119.3 20.1 %copy-start.67 = (f32[48]{0:T(128)}, f32[48]{0:T(128)S(1)}, u32[]{:S(2)}) copy-start(f32[48]{0:T(128)S(1)} %get-tuple-element.239) | copy-start | bytes 580
  119.3 20.1 %copy-start.68 = (f32[48]{0:T(128)}, f32[48]{0:T(128)S(1)}, u32[]{:S(2)}) copy-start(f32[48]{0:T(128)S(1)} %get-tuple-element.240) | copy-start | bytes 580
  119.6 16.3 %copy-start.15 = (f32[48,64]{1,0:T(8,128)}, f32[48,64]{1,0:T(8,128)S(1)}, u32[]{:S(2)}) copy-start(f32[48,64]{1,0:T(8,128)S(1)} %get-tuple-element.187) | copy-start | bytes 36868
  119.7 19.8 %copy-start.33 = (f32[48,64]{1,0:T(8,128)}, f32[48,64]{1,0:T(8,128)S(1)}, u32[]{:S(2)}) copy-start(f32[48,64]{1,0:T(8,128)S(1)} %get-tuple-element.183) | copy-start | bytes 36868
  119.7 19.8 %copy-start.34 = (f32[48,64]{1,0:T(8,128)}, f32[48,64]{1,0:T(8,128)S(1)}, u32[]{:S(2)}) copy-start(f32[48,64]{1,0:T(8,128)S(1)} %get-tuple-element.184) | copy-start | bytes 36868
  119.7 19.8 %copy-start.35 = (f32[48,64]{1,0:T(8,128)}, f32[48,64]{1,0:T(8,128)S(1)}, u32[]{:S(2)}) copy-start(f32[48,64]{1,0:T(8,128)S(1)} %get-tuple-element.185) | copy-start | bytes 36868
  164.5 197.4 %reduce-scatter.4.cloned.1.call-start = ((), (), s32[]{:S(2)}) async-start(), calls=%async_computation.4 | async-start | bytes 4423680
  264.6 14.8 %copy-start.69 = (f32[48]{0:T(128)}, f32[48]{0:T(128)S(1)}, u32[]{:S(2)}) copy-start(f32[48]{0:T(128)S(1)} %get-tuple-element.48) | copy-start | bytes 580
  264.6 14.8 %copy-start.70 = (f32[48]{0:T(128)}, f32[48]{0:T(128)S(1)}, u32[]{:S(2)}) copy-start(f32[48]{0:T(128)S(1)} %get-tuple-element.49) | copy-start | bytes 580
  264.7 14.8 %copy-start.71 = (f32[48]{0:T(128)}, f32[48]{0:T(128)S(1)}, u32[]{:S(2)}) copy-start(f32[48]{0:T(128)S(1)} %get-tuple-element.50) | copy-start | bytes 580
  267.5 11.9 %copy-start.26 = (f32[48,1,128]{2,1,0:T(1,128)}, f32[48,1,128]{2,1,0:T(1,128)S(1)}, u32[]{:S(2)}) copy-start(f32[48,1,128]{2,1,0:T(1,128)S(1)} %get-tuple-element.145) | copy-start | bytes 73732
  267.5 11.9 %copy-start.27 = (f32[48,1,128]{2,1,0:T(1,128)}, f32[48,1,128]{2,1,0:T(1,128)S(1)}, u32[]{:S(2)}) copy-start(f32[48,1,128]{2,1,0:T(1,128)S(1)} %get-tuple-element.146) | copy-start | bytes 73732
  275.9 12.8 %copy-start.8 = (bf16[48,8,1,1,64]{4,3,1,0,2:T(2,128)(2,1)S(1)}, bf16[48,8,1,1,64]{4,3,1,0,2:T(2,128)(2,1)}, u32[]{:S(2)}) copy-start(bf16[48,8,1,1,64]{4,3,1,0,2:T(2,128)(2,1)} %get-tuple-element.140) | copy-start | bytes 147460
  275.9 30.1 %copy-start.74 = (f32[64]{0:T(128)S(1)}, f32[64]{0:T(128)}, u32[]{:S(2)}) copy-start(f32[64]{0:T(128)} %get-tuple-element.209) | copy-start | bytes 772
  (58 other events, 344.6 us)
Sparse Core Ops, SparseCore 0:
  60.1 32.7 all-gather.6
  94.5 32.6 all-gather.4
  164.6 89.6 all-reduce.1
  316.4 45.5 reduce-scatter.3
where the time goes:
time: 374 us; the launch traced here: 372 us
  waiting for transfers between devices  110 us (29%)
  local copies, waits for them, and re-layouts  81.8 us (22%)
  other arithmetic  75.7 us (20%)
  blocking collectives  74.6 us (20%)
  between operations  15.4 us (4%)
  matrix products  14.1 us (4%)
    psum x1, waiting for transfers between devices, local(): total = lax.psum(term, 'heads')  85.9 us
    unnamed x181, local copies, waits for them, and re-layouts  55.4 us
    psum x2, blocking collectives, token_scale(): return rms_scale(lax.psum(local_sq, 'heads'), inner)  30.6 us
    select_n x2, other arithmetic, recur(): kept = jnp.where((accepted == t + 1)[:, None, None], state, kept)  17.3 us
    all_gather x1, blocking collectives, local(): lax.all_gather(conv_bc_state, 'heads', axis=3, tiled=True)  16.7 us
    unnamed x5, waiting for transfers between devices  16.4 us
    all_gather x1, blocking collectives, local(): lax.all_gather(conv_bc_w, 'heads', axis=2, tiled=True)  15.1 us
    unnamed x14, other arithmetic  12.3 us
  transfers between devices with their start and end apart: 4, of which 3 were waited for; matrix products, arithmetic and copies ran while one was open for 13% of the time, Pallas kernels for 0%

commit v1 on v0

--- a/solution.py
+++ b/solution.py
@@ -155,7 +155,17 @@
             term = (
                 jnp.dot(u_rows, out_w[layer], preferred_element_type=jnp.float32) * scale[:, None]
             )
-            total = lax.psum(term, "heads")
+
+            def lead_the_heads(packet, link_axis):
+                workers = lax.axis_size(link_axis)
+                aux = packet
+                for dev in [src_i for src_i in (1, 2, 4, 8, 16) if src_i < workers]:
+                    aux = aux + lax.ppermute(
+                        aux, link_axis, perm=[(rr, rr ^ dev) for rr in range(workers)]
+                    )
+                return aux
+
+            total = lead_the_heads(term, "heads")
             stream = (stream.astype(jnp.float32) + total).astype(jnp.bfloat16)
         else:
             mine = lax.psum_scatter(

time: 374 us -> 551 us (1.47)
  waiting for transfers between devices: 110 us -> 286 us
    ppermute x0 -> x3, waiting for transfers between devices: none -> 262 us  [lead_the_heads(): lax.ppermute(aux, link_axis, perm=[(rr, rr ^ dev) for rr in range(workers)])]
    psum x1 -> x0, waiting for transfers between devices: 85.9 us -> none  [local(): total = lax.psum(term, 'heads')]
    unnamed x5 -> x4, waiting for transfers between devices: 16.4 us -> 16.4 us
  transfers between devices with their start and end apart: 4 -> 6, of which waited for: 3 -> 5; matrix products, arithmetic and copies ran while one was open for 13% -> 9% of each run, Pallas kernels for 0% -> 0%
where the time goes in v1:
time: 551 us; the launch traced here: 548 us
  waiting for transfers between devices  286 us (52%)
  local copies, waits for them, and re-layouts  81.8 us (15%)
  other arithmetic  80.3 us (15%)
  blocking collectives  72.7 us (13%)
  between operations  15.4 us (3%)
  matrix products  12.2 us (2%)
    ppermute x3, waiting for transfers between devices, lead_the_heads(): lax.ppermute(aux, link_axis, perm=[(rr, rr ^ dev) for rr in range(workers)])  262 us
    unnamed x181, local copies, waits for them, and re-layouts  55.4 us
    psum x2, blocking collectives, token_scale(): return rms_scale(lax.psum(local_sq, 'heads'), inner)  28.8 us
    select_n x2, other arithmetic, recur(): kept = jnp.where((accepted == t + 1)[:, None, None], state, kept)  17.3 us
    all_gather x1, blocking collectives, local(): lax.all_gather(conv_bc_state, 'heads', axis=3, tiled=True)  16.7 us
    unnamed x4, waiting for transfers between devices  16.4 us
    all_gather x1, blocking collectives, local(): lax.all_gather(conv_bc_w, 'heads', axis=2, tiled=True)  15.1 us
    unnamed x14, other arithmetic  12.3 us
  transfers between devices with their start and end apart: 6, of which 5 were waited for; matrix products, arithmetic and copies ran while one was open for 9% of the time, Pallas kernels for 0%

profile of v1, /device:TPU:0, one launch (start us, length us, event | category | flops | bytes accessed | tf_op | source)
XLA Modules:
  0.0 548.3 jit_solution(18234454257303479747)
XLA Ops:
  7.2 43.7 %copy.113 = bf16[50280,320]{1,0:T(8,128)(2,1)} copy(bf16[50280,320]{0,1:T(8,128)(2,1)} %param.21) | data formatting | bytes 64358400 | tf_op args[2]
  51.2 7.8 %gather_fusion = bf16[384,320]{1,0:T(8,128)(2,1)S(1)} fusion(bf16[50280,320]{1,0:T(8,128)(2,1)} %copy.113, s32[1024]{0:T(1024)S(1)} %pad_clamp_fusion), kind=kCustom, calls=%fused_computation | custom fusion | bytes 493056 | tf_op jit(solution)/shard_map/gather | solution.py:147
  60.8 16.7 %all_gather.16 = bf16[2,48,3,256]{1,3,2,0:T(8,128)(2,1)S(1)} all-gather(bf16[2,48,3,32]{1,3,2,0:T(8,128)(2,1)S(1)} %copy-done.48), channel_id=1, replica_groups=mesh['batch'=4,'heads'=8] {'heads'}, dimensions={3}, use_global_device_ids=true | all-gather | bytes 165888 | tf_op jit(solution)/shard_map/all_gather | solution.py:91
  77.9 15.1 %all_gather.18 = bf16[2,4,256]{1,0,2:T(2,128)(2,1)S(1)} all-gather(bf16[2,4,32]{1,0,2:T(2,128)(2,1)S(1)} %copy.118), channel_id=1, replica_groups=mesh['batch'=4,'heads'=8] {'heads'}, dimensions={2}, use_global_device_ids=true | all-gather | bytes 4608 | tf_op jit(solution)/shard_map/all_gather | solution.py:89
  93.0 12.0 %all-gather.1 = bf16[8,32,2]{1,2,0:T(2,128)(2,1)S(1)} all-gather(bf16[1,32,2]{1,2,0:T(2,128)(2,1)S(1)} %bitcast.580), channel_id=1, replica_groups=mesh['batch'=4,'heads'=8] {'heads'}, dimensions={0}, use_global_device_ids=true | all-gather | bytes 1152 | tf_op jit(solution)/shard_map/all_gather | solution.py:90
  107.1 2.9 slice_reduce_fusion.7
  111.3 2.7 copy.115
  119.7 7.5 %all-gather.5.cloned.1.call-done = bf16[2,2560,256]{1,2,0:T(8,128)(2,1)} async-done(((bf16[2,2560,32]{1,2,0:T(8,128)(2,1)}), bf16[2,2560,256]{1,2,0:T(8,128)(2,1)}) %all-gather.5.cloned.1.call-update) | async-done | bytes 2621456 | tf_op jit(solution)/shard_map/all_gather | solution.py:88
  127.2 2.0 fusion.15
  131.2 4.1 multiply_add_fusion.8
  136.0 1.6 multiply_reduce_fusion.12
  139.5 3.7 multiply_reduce_fusion.8
  145.9 15.2 %psum.14 = f32[384]{0:T(512)S(1)} all-reduce(f32[384]{0:T(512)S(1)} %reshape.2511), channel_id=1, replica_groups=mesh['batch'=4,'heads'=8] {'heads'}, use_global_device_ids=true, to_apply=%region_10.11 | all-reduce | flops 384 | bytes 3072 | tf_op jit(solution)/shard_map/psum | solution.py:53
  162.9 6.8 %collective-permute-done = f32[384,2560]{1,0:T(8,128)S(1)} collective-permute-done((f32[384,2560]{1,0:T(8,128)S(1)}, f32[384,2560]{1,0:T(8,128)S(1)}, u32[]{:S(2)}, u32[]{:S(2)}) %collective-permute-start) | collective-permute-done | bytes 3932192 | tf_op jit(solution)/shard_map/ppermute | solution.py:163
  170.3 87.0 %collective-permute-done.1 = f32[384,2560]{1,0:T(8,128)S(1)} collective-permute-done((f32[384,2560]{1,0:T(8,128)S(1)}, f32[384,2560]{1,0:T(8,128)S(1)}, u32[]{:S(2)}, u32[]{:S(2)}) %collective-permute-start.1) | collective-permute-done | bytes 3932192 | tf_op jit(solution)/shard_map/ppermute | solution.py:163
  257.3 2.5 add.1165
  260.6 2.9 slice_reduce_fusion.3
  263.5 167.9 %collective-permute-done.2 = f32[384,2560]{1,0:T(8,128)} collective-permute-done((f32[384,2560]{1,0:T(8,128)}, f32[384,2560]{1,0:T(8,128)}, u32[]{:S(2)}, u32[]{:S(2)}) %collective-permute-start.2) | collective-permute-done | bytes 3932192 | tf_op jit(solution)/shard_map/ppermute | solution.py:163
  431.4 4.2 fusion.1
  443.0 2.1 fusion.14
  447.2 4.1 multiply_add_fusion.2
  452.5 1.6 multiply_reduce_fusion.4
  457.8 4.0 multiply_reduce_fusion
  465.3 1.9 constant_dynamic-update-slice_fusion.16
  468.9 13.6 %psum.15 = f32[384]{0:T(512)S(1)} all-reduce(f32[384]{0:T(512)S(1)} %reshape.2516), channel_id=1, replica_groups=mesh['batch'=4,'heads'=8] {'heads'}, use_global_device_ids=true, to_apply=%region_21.22 | all-reduce | flops 384 | bytes 3072 | tf_op jit(solution)/shard_map/psum | solution.py:53
  483.6 3.5 fusion
  487.1 5.6 %copy.139 = f32[2560,384]{1,0:T(8,128)} copy(f32[2560,384]{0,1:T(8,128)} %fusion) | data formatting | bytes 7864320
  494.0 1.7 fusion.105
  498.5 9.0 %select_select_fusion.1 = f32[1,48,1,64,128]{4,3,2,1,0:T(8,128)} fusion(f32[2,48,1,64,128]{4,3,2,1,0:T(8,128)S(1)} %copy-done.1, f32[48,128]{1,0:T(8,128)} %bitcast.536, f32[48,64]{1,0:T(8,128)} %copy-done.34, f32[48,128]{1,0:T(8,128)} %bitcast.534, f32[48,64]{1,0:T(8,128)} %copy-done.35, f32[48,128]{1,0:T(8,128)} %bitcast.532, f32[48,64]{1,0:T(8,128)} %copy-done.33, ...), kind=kLoop, calls=%fused_computation.22 | loop fusion | flops 12582912 | bytes 3442560 | tf_op jit(solution)/shard_map/vmap(jit(_where))/select_n | solution.py:41
  512.6 8.2 %select_select_fusion = f32[1,48,1,64,128]{4,3,2,1,0:T(8,128)S(1)} fusion(f32[2,48,1,64,128]{4,3,2,1,0:T(8,128)S(1)} %copy-done.1, f32[48,128]{1,0:T(8,128)} %bitcast.550, f32[48,64]{1,0:T(8,128)} %copy-done.40, f32[48,128]{1,0:T(8,128)} %bitcast.548, f32[48,64]{1,0:T(8,128)} %copy-done.42, f32[48,128]{1,0:T(8,128)} %bitcast.546, f32[48,64]{1,0:T(8,128)} %copy-done.41, ...), kind=kLoop, calls=%fused_computation.21 | loop fusion | flops 12582912 | bytes 3442560 | tf_op jit(solution)/shard_map/vmap(jit(_where))/select_n | solution.py:41
  520.9 1.9 pad_maximum_fusion
  522.8 15.7 %reduce-scatter.4.cloned.1.call-done = f32[320,384]{1,0:T(8,128)} async-done(((f32[2560,384]{1,0:T(8,128)}), f32[320,384]{1,0:T(8,128)}) %reduce-scatter.4.cloned.1.call-update) | async-done | bytes 491536
  (280 shorter events, 53.5 us)
Async XLA Ops:
  7.2 43.8 %copy-start.73 = (s32[48,8]{0,1:T(8,128)S(1)}, s32[48,8]{0,1:T(8,128)}, u32[]{:S(2)}) copy-start(s32[48,8]{0,1:T(8,128)} %param.19) | copy-start | bytes 4612
  7.2 104.1 %all-gather.7.cloned.1.call-start = ((), (), s32[]{:S(2)}) async-start(), calls=%async_computation.2 | async-start | bytes 2211840 | tf_op jit(solution)/shard_map/all_gather | solution.py:148
  59.0 18.7 %copy-start.75 = (bf16[2,4,32]{2,1,0:T(4,128)(2,1)S(1)}, bf16[2,4,32]{2,1,0:T(4,128)(2,1)}, u32[]{:S(2)}) copy-start(bf16[2,4,32]{2,1,0:T(4,128)(2,1)} %param.31) | copy-start | bytes 1540
  59.0 34.0 %copy-start.82 = (bf16[2,32]{1,0:T(2,128)(2,1)S(1)}, bf16[2,32]{1,0:T(2,128)(2,1)}, u32[]{:S(2)}) copy-start(bf16[2,32]{1,0:T(2,128)(2,1)} %param.32) | copy-start | bytes 388
  59.0 46.1 %copy-start.77 = (f32[2,1]{0,1:T(1,128)S(1)}, f32[2,1]{0,1:T(1,128)}, u32[]{:S(2)}) copy-start(f32[2,1]{0,1:T(1,128)} %param.26) | copy-start | bytes 28
  59.0 46.7 %copy-start.78 = (f32[2,1]{0,1:T(1,128)S(1)}, f32[2,1]{0,1:T(1,128)}, u32[]{:S(2)}) copy-start(f32[2,1]{0,1:T(1,128)} %param.27) | copy-start | bytes 28
  59.1 47.3 %copy-start.79 = (f32[2,1]{0,1:T(1,128)S(1)}, f32[2,1]{0,1:T(1,128)}, u32[]{:S(2)}) copy-start(f32[2,1]{0,1:T(1,128)} %param.28) | copy-start | bytes 28
  59.1 47.8 %copy-start.55 = (f32[2,2560]{1,0:T(2,128)S(1)}, f32[2,2560]{1,0:T(2,128)}, u32[]{:S(2)}) copy-start(f32[2,2560]{1,0:T(2,128)} %param.22) | copy-start | bytes 61444
  60.0 50.1 %copy-start.80 = (bf16[2,64]{1,0:T(2,128)(2,1)S(1)}, bf16[2,64]{1,0:T(2,128)(2,1)}, u32[]{:S(2)}) copy-start(bf16[2,64]{1,0:T(2,128)(2,1)} %param.30) | copy-start | bytes 772
  60.0 50.1 %copy-start.81 = (f32[2,64]{1,0:T(2,128)S(1)}, f32[2,64]{1,0:T(2,128)}, u32[]{:S(2)}) copy-start(f32[2,64]{1,0:T(2,128)} %param.33) | copy-start | bytes 1540
  60.0 51.2 %copy-start.76 = (bf16[2,4,64]{2,1,0:T(4,128)(2,1)S(1)}, bf16[2,4,64]{2,1,0:T(4,128)(2,1)}, u32[]{:S(2)}) copy-start(bf16[2,4,64]{2,1,0:T(4,128)(2,1)} %param.29) | copy-start | bytes 3076
  60.0 51.2 %copy-start.47 = (bf16[2,48,3,64]{3,1,2,0:T(8,128)(2,1)S(1)}, bf16[2,48,3,64]{3,1,2,0:T(8,128)(2,1)}, u32[]{:S(2)}) copy-start(bf16[2,48,3,64]{3,1,2,0:T(8,128)(2,1)} %param.36) | copy-start | bytes 110596
  60.0 67.2 %all-gather.5.cloned.1.call-start = ((), (), s32[]{:S(2)}) async-start(), calls=%async_computation.1 | async-start | bytes 2949120 | tf_op jit(solution)/shard_map/all_gather | solution.py:88
  60.8 477.7 %reduce-scatter.4.cloned.1.call-start = ((), (), s32[]{:S(2)}) async-start(), calls=%async_computation.3 | async-start | bytes 4423680
  77.8 51.5 %copy-start.10 = (bf16[48,3,256]{2,1,0:T(4,128)(2,1)}, bf16[48,3,256]{2,1,0:T(4,128)(2,1)S(1)}, u32[]{:S(2)}) copy-start(bf16[48,3,256]{2,1,0:T(4,128)(2,1)S(1)} %copy.117) | copy-start | bytes 221188
  111.3 327.5 %copy-start.17 = (bf16[48,3,64]{2,0,1:T(8,128)(2,1)}, bf16[48,3,64]{2,0,1:T(8,128)(2,1)S(1)}, u32[]{:S(2)}) copy-start(bf16[48,3,64]{2,0,1:T(8,128)(2,1)S(1)} %get-tuple-element.193) | copy-start | bytes 55300
  119.3 16.7 %copy-start.56 = (f32[48]{0:T(128)}, f32[48]{0:T(128)S(1)}, u32[]{:S(2)}) copy-start(f32[48]{0:T(128)S(1)} %get-tuple-element.236) | copy-start | bytes 580
  119.3 20.1 %copy-start.66 = (f32[48]{0:T(128)}, f32[48]{0:T(128)S(1)}, u32[]{:S(2)}) copy-start(f32[48]{0:T(128)S(1)} %get-tuple-element.238) | copy-start | bytes 580
  119.3 20.1 %copy-start.67 = (f32[48]{0:T(128)}, f32[48]{0:T(128)S(1)}, u32[]{:S(2)}) copy-start(f32[48]{0:T(128)S(1)} %get-tuple-element.239) | copy-start | bytes 580
  119.3 20.1 %copy-start.68 = (f32[48]{0:T(128)}, f32[48]{0:T(128)S(1)}, u32[]{:S(2)}) copy-start(f32[48]{0:T(128)S(1)} %get-tuple-element.240) | copy-start | bytes 580
  119.6 16.3 %copy-start.15 = (f32[48,64]{1,0:T(8,128)}, f32[48,64]{1,0:T(8,128)S(1)}, u32[]{:S(2)}) copy-start(f32[48,64]{1,0:T(8,128)S(1)} %get-tuple-element.187) | copy-start | bytes 36868
  119.7 19.8 %copy-start.33 = (f32[48,64]{1,0:T(8,128)}, f32[48,64]{1,0:T(8,128)S(1)}, u32[]{:S(2)}) copy-start(f32[48,64]{1,0:T(8,128)S(1)} %get-tuple-element.183) | copy-start | bytes 36868
  119.7 19.8 %copy-start.34 = (f32[48,64]{1,0:T(8,128)}, f32[48,64]{1,0:T(8,128)S(1)}, u32[]{:S(2)}) copy-start(f32[48,64]{1,0:T(8,128)S(1)} %get-tuple-element.184) | copy-start | bytes 36868
  119.7 19.8 %copy-start.35 = (f32[48,64]{1,0:T(8,128)}, f32[48,64]{1,0:T(8,128)S(1)}, u32[]{:S(2)}) copy-start(f32[48,64]{1,0:T(8,128)S(1)} %get-tuple-element.185) | copy-start | bytes 36868
  162.8 6.8 %collective-permute-start = (f32[384,2560]{1,0:T(8,128)S(1)}, f32[384,2560]{1,0:T(8,128)S(1)}, u32[]{:S(2)}, u32[]{:S(2)}) collective-permute-start(f32[384,2560]{1,0:T(8,128)S(1)} %convolution_multiply_fusion.1), channel_id=1, source_target_pairs={{0,1},{1,0},{2,3},{3,2},{4,5},{5,4},{6,7},{7,6},{8,9},{9,8},{10,11... | collective-permute-start | bytes 11796488 | tf_op jit(solution)/shard_map/ppermute | solution.py:163
  170.3 87.1 %collective-permute-start.1 = (f32[384,2560]{1,0:T(8,128)S(1)}, f32[384,2560]{1,0:T(8,128)S(1)}, u32[]{:S(2)}, u32[]{:S(2)}) collective-permute-start(f32[384,2560]{1,0:T(8,128)S(1)} %add.1164), channel_id=1, source_target_pairs={{0,2},{1,3},{2,0},{3,1},{4,6},{5,7},{6,4},{7,5},{8,10},{9,11},{10,... | collective-permute-start | bytes 11796488 | tf_op jit(solution)/shard_map/ppermute | solution.py:163
  259.8 171.6 %collective-permute-start.2 = (f32[384,2560]{1,0:T(8,128)}, f32[384,2560]{1,0:T(8,128)}, u32[]{:S(2)}, u32[]{:S(2)}) collective-permute-start(f32[384,2560]{1,0:T(8,128)} %add.1165), channel_id=1, source_target_pairs={{0,4},{1,5},{2,6},{3,7},{4,0},{5,1},{6,2},{7,3},{8,12},{9,13},{10,... | collective-permute-start | bytes 11796488 | tf_op jit(solution)/shard_map/ppermute | solution.py:163
  263.5 172.1 %copy-start.84 = (bf16[2,2560,1,128]{3,1,2,0:T(8,128)(2,1)S(1)}, bf16[2,2560,1,128]{3,1,2,0:T(8,128)(2,1)}, u32[]{:S(2)}) copy-start(bf16[2,2560,1,128]{3,1,2,0:T(8,128)(2,1)} %param.23) | copy-start | bytes 3932164
  442.9 14.8 %copy-start.69 = (f32[48]{0:T(128)}, f32[48]{0:T(128)S(1)}, u32[]{:S(2)}) copy-start(f32[48]{0:T(128)S(1)} %get-tuple-element.48) | copy-start | bytes 580
  442.9 14.8 %copy-start.70 = (f32[48]{0:T(128)}, f32[48]{0:T(128)S(1)}, u32[]{:S(2)}) copy-start(f32[48]{0:T(128)S(1)} %get-tuple-element.49) | copy-start | bytes 580
  443.0 14.8 %copy-start.71 = (f32[48]{0:T(128)}, f32[48]{0:T(128)S(1)}, u32[]{:S(2)}) copy-start(f32[48]{0:T(128)S(1)} %get-tuple-element.50) | copy-start | bytes 580
  454.2 28.3 %copy-start.74 = (f32[64]{0:T(128)S(1)}, f32[64]{0:T(128)}, u32[]{:S(2)}) copy-start(f32[64]{0:T(128)} %get-tuple-element.209) | copy-start | bytes 772
  (60 other events, 378.5 us)
Sparse Core Ops, SparseCore 0:
  60.1 32.7 all-gather.6
  94.5 32.6 all-gather.4
  492.9 45.5 reduce-scatter.3
